TPU v7x, 32 devices: a whole 2x2x4 slice. The times are simulated.
32 devices in a mesh: wa: 16 (over z, y, core), ha: 2 (over x).
Axes of the slice: x: 2, y: 2, z: 4, core: 2. Of those that a mesh axis runs over, the one named last changes fastest.
Arguments:
- tokens: bfloat16 [16384, 4096], P('wa'), may hold values from -6 to 6
- expert_ids: int32 [16384, 8], P('wa'), may hold values from 0 to 127, as said below
- keep_mask: int32 [16384, 8], P('wa'), may hold values from 0 to 1, as said below
- route_weight: float32 [16384, 8], P('wa'), may hold values from 0.2 to 1
- gate_weight: bfloat16 [4096, 1536], P('wa', 'ha'), may hold values from -0.09375 to 0.09375
- up_weight: bfloat16 [4096, 1536], P('wa', 'ha'), may hold values from -0.09375 to 0.09375
- down_weight: bfloat16 [4096, 1536], P('wa', 'ha'), may hold values from -0.15625 to 0.15625
Outputs:
- mixed: bfloat16 [16384, 4096], P('wa', 'ha')
Inputs may be any that keep to these rules, and one draw needn't show every extreme that they name: `expert_ids`: each row names 8 different experts. keep_mask[t, k] is 1 exactly where fewer than 128 earlier tokens of the same block of 1024 rows name expert_ids[t, k]; in some block 128 tokens naming expert 0 are kept.
All inputs are finite; a program needn't handle non-finite values.
Results may differ from a plain program's by a relative error of at most 0.005.
Values may be sent and summed in bfloat16 or wider, within the bound.
A program may use at most 128 MiB of HBM per device.

v0:
```python
import jax
import jax.numpy as jnp
from jax import lax
from jax.sharding import PartitionSpec as P

CAP = 128


def prefix(value, axis, join, neutral):
    count, mine = (lax.axis_size(axis), lax.axis_index(axis))
    pieces = lax.all_gather(value, axis)
    subtotal = jnp.full_like(value, 0) + jnp.asarray(neutral, value.dtype)

    def turn(position, subtotal):
        longer = join(subtotal, pieces[position])
        return jnp.where(position < mine, longer, subtotal)

    return lax.fori_loop(0, count - 1, turn, subtotal)


def add_counts(earlier, later):
    return earlier + later


def global_admit(chosen, position):
    counted = jnp.sum(chosen).reshape(1)
    earlier = prefix(counted, "wa", add_counts, jnp.zeros((1,), jnp.int32))
    capacity = lax.axis_size("wa") * CAP // 2
    return chosen * (earlier[0] + position < capacity).astype(jnp.int32)


def slot_table(position, marked):
    slot_ids = jnp.arange(CAP, dtype=jnp.int32)
    return (position[None, :] == slot_ids[:, None]) & (marked[None, :] == 1)


def run_expert(slot_rows, gate_weight, up_weight, down_weight):
    gate_next = jnp.dot(
        slot_rows,
        lax.all_gather(gate_weight, "wa", axis=0, tiled=True),
        preferred_element_type=jnp.float32,
    )
    up_next = jnp.dot(
        slot_rows,
        lax.all_gather(up_weight, "wa", axis=0, tiled=True),
        preferred_element_type=jnp.float32,
    )
    hidden = (jax.nn.silu(gate_next) * up_next).astype(jnp.bfloat16)
    return lax.dot_general(
        hidden,
        lax.all_gather(down_weight, "wa", axis=0, tiled=True),
        (((1,), (1,)), ((), ())),
        preferred_element_type=jnp.float32,
    )


def per_device(tokens, expert_ids, keep_mask, route_weight, gate_weight, up_weight, down_weight):
    matches = (expert_ids == 0) & (keep_mask == 1)
    chosen = jnp.any(matches, axis=1).astype(jnp.int32)
    route_sum = jnp.sum(jnp.where(matches, route_weight, jnp.float32(0.0)), axis=1)
    position = jnp.cumsum(chosen) - chosen
    admitted = global_admit(chosen, position)
    dispatch = slot_table(position, admitted)
    slot_rows = jnp.dot(
        dispatch.astype(jnp.bfloat16), tokens, preferred_element_type=jnp.float32
    ).astype(jnp.bfloat16)
    expert_out = run_expert(slot_rows, gate_weight, up_weight, down_weight)
    final_table = slot_table(position, admitted)
    combine_map = jnp.where(final_table.T, route_sum[:, None], jnp.float32(0.0))
    halves = lax.psum_scatter(expert_out, "ha", scatter_dimension=1, tiled=True)
    mixed = jnp.dot(
        combine_map, halves, precision=lax.Precision.HIGHEST, preferred_element_type=jnp.float32
    )
    return mixed.astype(jnp.bfloat16)


def solution(mesh):
    return jax.shard_map(
        per_device,
        mesh=mesh,
        in_specs=(
            P("wa", None),
            P("wa", None),
            P("wa", None),
            P("wa", None),
            P("wa", "ha"),
            P("wa", "ha"),
            P("wa", "ha"),
        ),
        out_specs=P("wa", "ha"),
        check_vma=False,
    )
```

profile of v0, /device:TPU:0, one launch (start us, length us, event | category | flops | bytes accessed | tf_op | source)
XLA Modules:
  0.0 254.8 jit_solution(10121087111049697661)
XLA Ops:
  6.5 0.0 all-gather.4.cloned.1.call-start
  6.5 0.7 all-gather.4.cloned.1.call-update
  7.3 0.0 all-gather.6.cloned.1.call-start
  7.3 0.7 all-gather.6.cloned.1.call-update
  8.0 0.0 all-gather.8.cloned.1.call-start
  8.1 0.7 all-gather.8.cloned.1.call-update
  8.7 0.0 reduce-scatter.2.cloned.1.call-start
  8.8 0.8 select_reduce_fusion
  9.6 1.2 dynamic-slice
  10.9 0.7 convert_reduce_fusion
  11.6 1.3 dynamic-update-slice
  12.9 14.4 %all-reduce = s32[16]{0:T(128)S(1)} all-reduce(s32[16]{0:T(128)S(1)} %dynamic-update-slice), channel_id=1, replica_groups=mesh['wa'=16,'ha'=2] {'wa'}, use_global_device_ids=true, to_apply=%add | all-reduce | flops 16 | bytes 128
  27.3 0.3 reduce-window.9
  27.5 0.1 slice.7
  27.6 18.4 %while.13 = (s32[]{:T(128)}, s32[1]{0:T(128)}, s32[]{:T(128)}, s32[16,1]{0,1:T(1,128)S(1)}, s32[]{:T(128)}) while((s32[]{:T(128)}, s32[1]{0:T(128)}, s32[]{:T(128)}, s32[16,1]{0,1:T(1,128)S(1)}, s32[]{:T(128)}) %tuple.41), condition=%wide.region_5.6_spmd, body=%wide.region_4.5_spmd.sunk | while | flops 5 | bytes 107 | solution.py:18
  27.6 0.6 constant_dynamic-slice_fusion.2
  28.9 0.6 constant_dynamic-slice_fusion.2
  30.1 0.6 constant_dynamic-slice_fusion.2
  31.3 0.6 constant_dynamic-slice_fusion.2
  32.6 0.6 constant_dynamic-slice_fusion.2
  33.8 0.6 constant_dynamic-slice_fusion.2
  35.0 0.6 constant_dynamic-slice_fusion.2
  36.3 0.6 constant_dynamic-slice_fusion.2
  37.5 0.6 constant_dynamic-slice_fusion.2
  38.7 0.6 constant_dynamic-slice_fusion.2
  39.9 0.6 constant_dynamic-slice_fusion.2
  41.2 0.6 constant_dynamic-slice_fusion.2
  42.4 0.6 constant_dynamic-slice_fusion.2
  43.6 0.6 constant_dynamic-slice_fusion.2
  44.9 0.6 constant_dynamic-slice_fusion.2
  46.1 0.1 slice_reduce_fusion
  46.2 0.1 fusion.19
  46.3 4.7 %convolution_convert_fusion = bf16[128,4096]{1,0:T(8,128)(2,1)S(1)} fusion(bf16[1024,4096]{1,0:T(8,128)(2,1)} %param.9, s32[1024]{0:T(1024)S(1)} %get-tuple-element.96, pred[1024]{0:T(1024)(128)(4,1)S(1)} %get-tuple-element.95), kind=kOutput, calls=%fused_computation.1 | convolution fusion | flops 1074528256 | bytes 9442304 | tf_op jit(solution)/shard_map/dot_general | solution.py:64
  51.0 22.8 %all-gather.4.cloned.1.call-done = bf16[4096,768]{1,0:T(8,128)(2,1)} async-done(((bf16[256,768]{1,0:T(8,128)(2,1)}), bf16[4096,768]{1,0:T(8,128)(2,1)}) %all-gather.4.cloned.1.call-update) | async-done | bytes 6291472 | tf_op jit(solution)/shard_map/all_gather | solution.py:40
  73.8 3.8 %fusion.22 = f32[128,768]{1,0:T(8,128)S(1)} fusion(bf16[128,4096]{1,0:T(8,128)(2,1)S(1)} %convolution_convert_fusion, bf16[4096,768]{1,0:T(8,128)(2,1)} %all-gather.4.cloned.1.call-done), kind=kOutput, calls=%fused_computation.34 | convolution fusion | flops 805306368 | bytes 7733248 | tf_op jit(solution)/shard_map/dot_general | solution.py:38
  77.6 58.6 %all-gather.6.cloned.1.call-done = bf16[4096,768]{1,0:T(8,128)(2,1)} async-done(((bf16[256,768]{1,0:T(8,128)(2,1)}), bf16[4096,768]{1,0:T(8,128)(2,1)}) %all-gather.6.cloned.1.call-update) | async-done | bytes 6291472 | tf_op jit(solution)/shard_map/all_gather | solution.py:45
  136.2 62.4 %all-gather.8.cloned.1.call-done = bf16[4096,768]{1,0:T(8,128)(2,1)} async-done(((bf16[256,768]{1,0:T(8,128)(2,1)}), bf16[4096,768]{1,0:T(8,128)(2,1)}) %all-gather.8.cloned.1.call-update) | async-done | bytes 6291472 | tf_op jit(solution)/shard_map/all_gather | solution.py:51
  198.7 9.0 %fusion.1 = f32[128,4096]{1,0:T(8,128)} fusion(bf16[4096,768]{1,0:T(8,128)(2,1)} %all-gather.8.cloned.1.call-done, bf16[128,4096]{1,0:T(8,128)(2,1)S(1)} %convolution_convert_fusion, bf16[4096,768]{1,0:T(8,128)(2,1)} %all-gather.6.cloned.1.call-done, f32[128,768]{1,0:T(8,128)S(1)} %fusion.22), kind=kOutput, calls=%fused_computation.5 | convolution fusion | flops 1611202560 | bytes 16121856 | tf_op jit(solution)/shard_map/dot_general | solution.py:49
  207.7 0.0 reduce-scatter.2.cloned.1.call-update
  207.7 30.7 %reduce-scatter.2.cloned.1.call-done = f32[128,2048]{1,0:T(8,128)} async-done(((f32[128,4096]{1,0:T(8,128)}), f32[128,2048]{1,0:T(8,128)}) %reduce-scatter.2.cloned.1.call-update) | async-done | bytes 1048592 | tf_op jit(solution)/shard_map/reduce_scatter | solution.py:70
  238.4 9.9 %convolution_convert_fusion.1 = bf16[1024,2048]{1,0:T(8,128)(2,1)} fusion(f32[128,2048]{1,0:T(8,128)} %reduce-scatter.2.cloned.1.call-done, f32[1024]{0:T(1024)S(1)} %get-tuple-element.93, s32[1024]{0:T(1024)S(1)} %get-tuple-element.96, pred[1024]{0:T(1024)(128)(4,1)S(1)} %get-tuple-element.95), kind=kOutput, calls=%fused_computation.2 | convolution fusion | flops 3223715840 | bytes 5252096 | tf_op jit(solution)/shard_map/dot_general | solution.py:71
  (4 shorter events, 0.1 us)
Async XLA Ops:
  6.5 67.3 %all-gather.4.cloned.1.call-start = ((), (), s32[]{:S(2)}) async-start(), calls=%async_computation.1 | async-start | bytes 6684672 | tf_op jit(solution)/shard_map/all_gather | solution.py:40
  7.3 129.0 %all-gather.6.cloned.1.call-start = ((), (), s32[]{:S(2)}) async-start(), calls=%async_computation.2 | async-start | bytes 6684672 | tf_op jit(solution)/shard_map/all_gather | solution.py:45
  8.0 190.6 %all-gather.8.cloned.1.call-start = ((), (), s32[]{:S(2)}) async-start(), calls=%async_computation.3 | async-start | bytes 6684672 | tf_op jit(solution)/shard_map/all_gather | solution.py:51
  8.7 229.7 %reduce-scatter.2.cloned.1.call-start = ((), (), s32[]{:S(2)}) async-start(), calls=%async_computation.4 | async-start | bytes 3145728 | tf_op jit(solution)/shard_map/reduce_scatter | solution.py:70
Sparse Core Ops, SparseCore 0:
  9.6 64.1 all-gather.3
  76.1 60.0 all-gather.5
  138.5 60.0 all-gather.7
  207.8 30.5 reduce-scatter.1
where the time goes:
time: 255 us
  waiting for transfers between devices  177 us (69%)
  matrix products  27.4 us (11%)
  blocking collectives  14.4 us (6%)
  between operations  13.2 us (5%)
  local copies, waits for them, and re-layouts  11.6 us (5%)
  loops' own time  9.59 us (4%)
    all_gather x1, waiting for transfers between devices, run_expert(): lax.all_gather(down_weight, 'wa', axis=0, tiled=True)  62.4 us
    all_gather x1, waiting for transfers between devices, run_expert(): lax.all_gather(up_weight, 'wa', axis=0, tiled=True)  58.6 us
    reduce_scatter x1, waiting for transfers between devices, per_device(): halves = lax.psum_scatter(expert_out, 'ha', scatter_dimension=1, tiled=True)  30.7 us
    all_gather x1, waiting for transfers between devices, run_expert(): lax.all_gather(gate_weight, 'wa', axis=0, tiled=True)  22.8 us
    unnamed x1, blocking collectives  14.4 us
    dot_general x1, matrix products, per_device(): jnp.dot(combine_map, halves, precision=lax.Precision.HIGHEST, preferred_e...  9.87 us
    another operation x1, loops' own time, prefix(): return lax.fori_loop(0, count - 1, turn, subtotal)  9.59 us
    dot_general x1, matrix products, run_expert(): lax.dot_general(hidden, lax.all_gather(down_weight, 'wa', axis=0, tiled=T...  9.02 us
  transfers between devices with their start and end apart: 4, of which 4 were waited for; matrix products, arithmetic and copies ran while one was open for 9% of the time, Pallas kernels for 0%

commit v1 on v0

--- a/solution.py
+++ b/solution.py
@@ -4,6 +4,18 @@
 from jax.sharding import PartitionSpec as P
 
 CAP = 128
+
+
+def attach_the_axis_part(target):
+    return jnp.concatenate(
+        jax.lax.all_to_all(
+            jnp.stack([target for _ in range(jax.lax.axis_size("wa"))]),
+            axis_name="wa",
+            split_axis=0,
+            concat_axis=0,
+        ),
+        0,
+    )
 
 
 def prefix(value, axis, join, neutral):
@@ -36,9 +48,7 @@
 
 def run_expert(slot_rows, gate_weight, up_weight, down_weight):
     gate_next = jnp.dot(
-        slot_rows,
-        lax.all_gather(gate_weight, "wa", axis=0, tiled=True),
-        preferred_element_type=jnp.float32,
+        slot_rows, attach_the_axis_part(gate_weight), preferred_element_type=jnp.float32
     )
     up_next = jnp.dot(
         slot_rows,

time: 255 us -> 298 us (1.17)
  blocking collectives: 14.4 us -> 191 us
  waiting for transfers between devices: 177 us -> 33.5 us
  starting transfers between devices: 0.12 us -> 7.68 us
  local copies, waits for them, and re-layouts: 11.6 us -> 14.9 us
    unnamed x1, blocking collectives: 14.4 us -> 191 us
    all_gather x1, waiting for transfers between devices: 62.4 us -> 0.02 us  [run_expert(): lax.all_gather(down_weight, 'wa', axis=0, tiled=True)]
    all_gather x1, waiting for transfers between devices: 58.6 us -> 0.02 us  [run_expert(): lax.all_gather(up_weight, 'wa', axis=0, tiled=True)]
    all_gather x1 -> x0, waiting for transfers between devices: 22.8 us -> none  [run_expert(): lax.all_gather(gate_weight, 'wa', axis=0, tiled=True)]
    all_to_all x0 -> x1, starting transfers between devices: none -> 7.6 us  [attach_the_axis_part(): jax.lax.all_to_all(jnp.stack([target for _ in range(jax.lax.axis_size('wa...]
    another operation x1 -> x2, local copies, waits for them, and re-layouts: 0.11 us -> 4.32 us  [the longest x1 4.2 us: attach_the_axis_part(): jnp.stack([target for _ in range(jax.lax.axis_size('wa'))])]
  transfers between devices with their start and end apart: 4 -> 4, of which waited for: 4 -> 1; matrix products, arithmetic and copies ran while one was open for 9% -> 8% of each run, Pallas kernels for 0% -> 0%
where the time goes in v1:
time: 298 us
  blocking collectives  191 us (64%)
  waiting for transfers between devices  33.5 us (11%)
  matrix products  27.4 us (9%)
  local copies, waits for them, and re-layouts  14.9 us (5%)
  between operations  13.2 us (4%)
  loops' own time  8.75 us (3%)
  starting transfers between devices  7.68 us (3%)
    unnamed x1, blocking collectives  191 us
    reduce_scatter x1, waiting for transfers between devices, per_device(): halves = lax.psum_scatter(expert_out, 'ha', scatter_dimension=1, tiled=True)  32 us
    dot_general x1, matrix products, per_device(): jnp.dot(combine_map, halves, precision=lax.Precision.HIGHEST, preferred_e...  9.87 us
    dot_general x1, matrix products, run_expert(): lax.dot_general(hidden, lax.all_gather(down_weight, 'wa', axis=0, tiled=T...  9.02 us
    another operation x1, loops' own time, prefix(): return lax.fori_loop(0, count - 1, turn, subtotal)  8.75 us
    dynamic_slice x15, local copies, waits for them, and re-layouts, turn(): longer = join(subtotal, pieces[position])  8.66 us
    all_to_all x1, starting transfers between devices, attach_the_axis_part(): jax.lax.all_to_all(jnp.stack([target for _ in range(jax.lax.axis_size('wa...  7.6 us
  transfers between devices with their start and end apart: 4, of which 1 were waited for; matrix products, arithmetic and copies ran while one was open for 8% of the time, Pallas kernels for 0%

profile of v1, /device:TPU:0, one launch (start us, length us, event | category | flops | bytes accessed | tf_op | source)
XLA Modules:
  0.0 297.8 jit_solution(1920746839595108730)
XLA Ops:
  6.5 0.0 all-gather.3.cloned.1.call-start
  6.5 0.7 all-gather.3.cloned.1.call-update
  7.3 4.2 %stack.2 = bf16[16,256,768]{2,1,0:T(8,128)(2,1)} broadcast(bf16[256,768]{1,0:T(8,128)(2,1)} %param.13), dimensions={1,2} | broadcast | bytes 6684672 | tf_op jit(solution)/shard_map/stack | solution.py:12
  11.5 0.0 copy-start
  11.5 0.0 copy-start.1
  11.5 0.0 copy-start.2
  11.5 0.0 copy-start.3
  11.5 7.6 %all-to-all-start = ((bf16[16,256,768]{2,1,0:T(8,128)(2,1)}), bf16[16,256,768]{2,1,0:T(8,128)(2,1)}, u32[]{:S(2)}, u32[]{:S(2)}) async-start(bf16[16,256,768]{2,1,0:T(8,128)(2,1)} %stack.2), calls=%async_computation | async-start | bytes 12582912 | tf_op jit(solution)/shard_map/all_to_all | solution.py:11
  19.1 0.0 all-gather.5.cloned.1.call-start
  19.1 0.7 all-gather.5.cloned.1.call-update
  19.8 0.0 reduce-scatter.2.cloned.1.call-start
  19.9 0.0 copy-done
  19.9 0.0 copy-done.1
  19.9 0.0 copy-done.2
  20.0 0.0 copy-done.3
  20.0 0.6 dynamic-slice
  20.6 0.6 convert_reduce_fusion
  21.2 1.3 dynamic-update-slice
  22.5 191.2 %all-reduce = s32[16]{0:T(128)S(1)} all-reduce(s32[16]{0:T(128)S(1)} %dynamic-update-slice), channel_id=1, replica_groups=mesh['wa'=16,'ha'=2] {'wa'}, use_global_device_ids=true, to_apply=%add | all-reduce | flops 16 | bytes 128
  213.7 0.3 reduce-window.9
  214.0 0.1 slice.7
  214.1 17.4 %while.13 = (s32[]{:T(128)}, s32[1]{0:T(128)}, s32[]{:T(128)}, s32[16,1]{0,1:T(1,128)S(1)}, s32[]{:T(128)}) while((s32[]{:T(128)}, s32[1]{0:T(128)}, s32[]{:T(128)}, s32[16,1]{0,1:T(1,128)S(1)}, s32[]{:T(128)}) %tuple.39), condition=%wide.region_5.6_spmd, body=%wide.region_4.5_spmd.sunk | while | flops 5 | bytes 107 | solution.py:30
  214.1 0.6 constant_dynamic-slice_fusion.2
  215.3 0.6 constant_dynamic-slice_fusion.2
  216.4 0.6 constant_dynamic-slice_fusion.2
  217.6 0.6 constant_dynamic-slice_fusion.2
  218.8 0.6 constant_dynamic-slice_fusion.2
  219.9 0.6 constant_dynamic-slice_fusion.2
  221.1 0.6 constant_dynamic-slice_fusion.2
  222.2 0.6 constant_dynamic-slice_fusion.2
  223.4 0.6 constant_dynamic-slice_fusion.2
  224.6 0.6 constant_dynamic-slice_fusion.2
  225.7 0.6 constant_dynamic-slice_fusion.2
  226.9 0.6 constant_dynamic-slice_fusion.2
  228.1 0.6 constant_dynamic-slice_fusion.2
  229.2 0.6 constant_dynamic-slice_fusion.2
  230.4 0.6 constant_dynamic-slice_fusion.2
  231.5 0.1 slice_reduce_fusion
  231.6 0.1 fusion.19
  231.7 4.7 %convolution_convert_fusion = bf16[128,4096]{1,0:T(8,128)(2,1)S(1)} fusion(bf16[1024,4096]{1,0:T(8,128)(2,1)} %param.9, s32[1024]{0:T(1024)S(1)} %get-tuple-element.96, pred[1024]{0:T(1024)(128)(4,1)S(1)} %get-tuple-element.95), kind=kOutput, calls=%fused_computation.1 | convolution fusion | flops 1074528256 | bytes 9442304 | tf_op jit(solution)/shard_map/dot_general | solution.py:74
  236.5 0.0 all-to-all-done
  236.5 3.8 %fusion.22 = f32[128,768]{1,0:T(8,128)S(1)} fusion(bf16[128,4096]{1,0:T(8,128)(2,1)S(1)} %convolution_convert_fusion, bf16[4096,768]{1,0:T(8,128)(2,1)} %bitcast.8), kind=kOutput, calls=%fused_computation.34 | convolution fusion | flops 805306368 | bytes 7733248 | tf_op jit(solution)/shard_map/dot_general | solution.py:50
  240.3 0.0 all-gather.3.cloned.1.call-done
  240.3 0.0 all-gather.5.cloned.1.call-done
  240.4 9.0 %fusion.1 = f32[128,4096]{1,0:T(8,128)} fusion(bf16[4096,768]{1,0:T(8,128)(2,1)} %all-gather.5.cloned.1.call-done, bf16[128,4096]{1,0:T(8,128)(2,1)S(1)} %convolution_convert_fusion, bf16[4096,768]{1,0:T(8,128)(2,1)} %all-gather.3.cloned.1.call-done, f32[128,768]{1,0:T(8,128)S(1)} %fusion.22), kind=kOutput, calls=%fused_computation.5 | convolution fusion | flops 1611202560 | bytes 16121856 | tf_op jit(solution)/shard_map/dot_general | solution.py:59
  249.4 0.0 reduce-scatter.2.cloned.1.call-update
  249.4 32.0 %reduce-scatter.2.cloned.1.call-done = f32[128,2048]{1,0:T(8,128)} async-done(((f32[128,4096]{1,0:T(8,128)}), f32[128,2048]{1,0:T(8,128)}) %reduce-scatter.2.cloned.1.call-update) | async-done | bytes 1048592 | tf_op jit(solution)/shard_map/reduce_scatter | solution.py:80
  281.4 9.9 %convolution_convert_fusion.1 = bf16[1024,2048]{1,0:T(8,128)(2,1)} fusion(f32[128,2048]{1,0:T(8,128)} %reduce-scatter.2.cloned.1.call-done, f32[1024]{0:T(1024)S(1)} %get-tuple-element.93, s32[1024]{0:T(1024)S(1)} %get-tuple-element.96, pred[1024]{0:T(1024)(128)(4,1)S(1)} %get-tuple-element.95), kind=kOutput, calls=%fused_computation.2 | convolution fusion | flops 3223715840 | bytes 5252096 | tf_op jit(solution)/shard_map/dot_general | solution.py:81
  (5 shorter events, 0.1 us)
Async XLA Ops:
  6.5 233.8 %all-gather.3.cloned.1.call-start = ((), (), s32[]{:S(2)}) async-start(), calls=%async_computation.2 | async-start | bytes 6684672 | tf_op jit(solution)/shard_map/all_gather | solution.py:55
  11.5 8.4 %copy-start = (f32[1024,8]{0,1:T(8,128)S(1)}, f32[1024,8]{0,1:T(8,128)}, u32[]{:S(2)}) copy-start(f32[1024,8]{0,1:T(8,128)} %param.12) | copy-start | bytes 98308
  11.5 8.4 %copy-start.1 = (s32[1024,8]{0,1:T(8,128)S(1)}, s32[1024,8]{0,1:T(8,128)}, u32[]{:S(2)}) copy-start(s32[1024,8]{0,1:T(8,128)} %param.11) | copy-start | bytes 98308
  11.5 8.4 %copy-start.2 = (s32[1024,8]{0,1:T(8,128)S(1)}, s32[1024,8]{0,1:T(8,128)}, u32[]{:S(2)}) copy-start(s32[1024,8]{0,1:T(8,128)} %param.10) | copy-start | bytes 98308
  11.5 8.5 %copy-start.3 = (u32[32]{0:T(128)S(1)}, u32[32]{0:T(128)}, u32[]{:S(2)}) copy-start(u32[32]{0:T(128)} %constant.51) | copy-start | bytes 388
  11.5 225.0 %all-to-all-start = ((bf16[16,256,768]{2,1,0:T(8,128)(2,1)}), bf16[16,256,768]{2,1,0:T(8,128)(2,1)}, u32[]{:S(2)}, u32[]{:S(2)}) async-start(bf16[16,256,768]{2,1,0:T(8,128)(2,1)} %stack.2), calls=%async_computation | async-start | bytes 12582912 | tf_op jit(solution)/shard_map/all_to_all | solution.py:11
  19.1 221.3 %all-gather.5.cloned.1.call-start = ((), (), s32[]{:S(2)}) async-start(), calls=%async_computation.3 | async-start | bytes 6684672 | tf_op jit(solution)/shard_map/all_gather | solution.py:61
  19.8 261.6 %reduce-scatter.2.cloned.1.call-start = ((), (), s32[]{:S(2)}) async-start(), calls=%async_computation.4 | async-start | bytes 3145728 | tf_op jit(solution)/shard_map/reduce_scatter | solution.py:80
Sparse Core Ops, SparseCore 0:
  9.6 149.9 all-gather.2
  161.9 75.8 all-gather.4
  249.5 31.8 reduce-scatter.1
